TPU v7x, 32 devices: a whole 2x2x4 slice. The times are simulated.
32 devices in a mesh: dp: 16 (over z, x, core), mp: 2 (over y).
Axes of the slice: x: 2, y: 2, z: 4, core: 2. Of those that a mesh axis runs over, the one named last changes fastest.
Arguments:
- tokens: bfloat16 [8192, 8192], P('dp'), may hold values from -6 to 6
- queries: bfloat16 [8192, 64, 128], P('dp', 'mp'), may hold values from -68 to 68
- out_grad: bfloat16 [8192, 64, 128], P('dp', 'mp'), may hold values from -6 to 6
- segment_ids: int32 [16, 512], P('dp'), may hold values from 0 to 3, never falling along the last dimension, each value on 1 to 256 neighbouring positions
- weight_slots: bfloat16 [16384, 8, 2, 128], P('dp', 'mp'), may hold values from -0.0625 to 0.0625
- old_place: int32 [64], replicated, may hold values from 0 to 127, as said below
- new_place: int32 [64], replicated, may hold values from 0 to 127, as said below
Outputs:
- input_grad: bfloat16 [8192, 8192], P('dp', 'mp')
- query_grad: bfloat16 [8192, 64, 128], P('dp', 'mp')
- weight_grad: float32 [16384, 8, 2, 128], P('dp', 'mp')
Inputs may be any that keep to these rules, and one draw needn't show every extreme that they name: `old_place`: entries are distinct slot numbers; slot s lies on index s // 8 of dp; some index of dp holds 8 blocks. `new_place`: entries are distinct slot numbers; slot s lies on index s // 8 of dp; some index of dp receives 8 blocks.
All inputs are finite; a program needn't handle non-finite values.
Results may differ from a plain program's by a relative error of at most 0.018.
Values may be sent and summed in bfloat16 or wider, within the bound.
No kernel may reach another device: no remote copies, remote signals or barrier semaphores. Data moves between devices by JAX's collectives and lax.ppermute only.
A program may use at most 192 MiB of HBM per device.

v0:
```python
import jax
import jax.numpy as jnp
from jax import lax
from jax.sharding import PartitionSpec as P

BR = 128


def attend(tokens, weights, queries, out_grad, seg_row):
    tok_count = tokens.shape[0]
    model_width = weights.shape[0]
    head_count = weights.shape[1]
    head_size = weights.shape[3]
    per_head = queries.shape[1] // head_count
    half_size = head_size // 2
    projected = jnp.dot(
        tokens,
        weights.reshape(model_width, head_count * 2 * head_size),
        preferred_element_type=jnp.float32,
    )
    projected = projected.reshape(tok_count, head_count, 2, head_size)
    frequency = 500000.0 ** (-2.0 * jnp.arange(half_size, dtype=jnp.float32) / head_size)
    angle_tab = jnp.arange(tok_count, dtype=jnp.float32)[:, None] * frequency[None, :]
    cos_tab = jnp.cos(angle_tab)[:, None, :]
    sin_tab = jnp.sin(angle_tab)[:, None, :]
    lower_half = projected[:, :, 0, :half_size]
    upper_half = projected[:, :, 0, half_size:]
    rot_keys = jnp.concatenate(
        [lower_half * cos_tab - upper_half * sin_tab, upper_half * cos_tab + lower_half * sin_tab],
        axis=-1,
    ).astype(jnp.bfloat16)
    values = projected[:, :, 1].astype(jnp.bfloat16)
    inv_root = 1.0 / jnp.sqrt(jnp.float32(head_size))
    query_wide = queries.reshape(tok_count, head_count, per_head, head_size).astype(jnp.float32)
    outgrad_wide = out_grad.reshape(tok_count, head_count, per_head, head_size).astype(jnp.float32)
    key_wide = rot_keys.astype(jnp.float32)
    value_wide = values.astype(jnp.float32)
    scores = jnp.einsum("qhgd,khd->hgqk", query_wide, key_wide) * inv_root
    position = jnp.arange(tok_count)
    allowed = (position[:, None] >= position[None, :]) & (seg_row[:, None] == seg_row[None, :])
    scores = jnp.where(allowed, scores, jnp.float32(-1e30))
    row_max = jnp.max(scores, axis=-1, keepdims=True)
    exp_scores = jnp.exp(scores - row_max)
    attn_prob = exp_scores / jnp.sum(exp_scores, axis=-1, keepdims=True)
    prob_half = lax.optimization_barrier(attn_prob.astype(jnp.bfloat16)).astype(jnp.float32)
    attn_out = jnp.einsum("hgqk,khd->qhgd", prob_half, value_wide)
    row_dot = jnp.sum(outgrad_wide * attn_out, axis=-1)
    prob_grad = jnp.einsum("qhgd,khd->hgqk", outgrad_wide, value_wide)
    score_grad = attn_prob * (prob_grad - jnp.transpose(row_dot, (1, 2, 0))[..., None])
    score_half = lax.optimization_barrier(score_grad.astype(jnp.bfloat16)).astype(jnp.float32)
    query_grad = (
        (jnp.einsum("hgqk,khd->qhgd", score_half, key_wide) * inv_root)
        .reshape(tok_count, head_count * per_head, head_size)
        .astype(jnp.bfloat16)
    )
    rot_grad = jnp.einsum("hgqk,qhgd->khd", score_half, query_wide) * inv_root
    value_grad = jnp.einsum("hgqk,qhgd->khd", prob_half, outgrad_wide)
    grad_lower = rot_grad[..., :half_size]
    grad_upper = rot_grad[..., half_size:]
    key_grad = jnp.concatenate(
        [grad_lower * cos_tab + grad_upper * sin_tab, grad_upper * cos_tab - grad_lower * sin_tab],
        axis=-1,
    )
    pair_grad = jnp.stack([key_grad, value_grad], axis=2).astype(jnp.bfloat16)
    return (query_grad, pair_grad)


def pick_blocks(selector, source, block_rows):
    block_total = source.shape[0] // block_rows
    flat = source.reshape(block_total, -1)
    picked = jnp.dot(selector.astype(jnp.bfloat16), flat, preferred_element_type=jnp.float32)
    return picked


def local(tokens, queries, out_grad, segment_ids, weight_slots, old_place, new_place):
    tok_count = tokens.shape[0]
    slot_rows = weight_slots.shape[0]
    head_count = weight_slots.shape[1]
    head_size = weight_slots.shape[3]
    block_rows = BR
    slot_count = slot_rows // block_rows
    dp_count = lax.axis_size("dp")
    slot_total = dp_count * slot_count
    block_count = old_place.shape[0]
    gathered = lax.all_gather(weight_slots, "dp", axis=0, tiled=True)
    all_slots = jnp.arange(slot_total, dtype=jnp.int32)
    old_pick = (old_place[:, None] == all_slots[None, :]).astype(jnp.int32)
    weights = pick_blocks(old_pick, gathered, block_rows).astype(jnp.bfloat16)
    weights = weights.reshape(block_count * block_rows, head_count, 2, head_size)
    query_grad, pair_grad = attend(tokens, weights, queries, out_grad, segment_ids[0])
    pair_flat = pair_grad.reshape(tok_count, head_count * 2 * head_size)
    seq_part = lax.dot_general(
        tokens, pair_flat, (((0,), (0,)), ((), ())), preferred_element_type=jnp.float32
    ).astype(jnp.bfloat16)
    slot_ids = jnp.arange(slot_total, dtype=jnp.int32)
    matched = (new_place[None, :] == slot_ids[:, None]).astype(jnp.bfloat16)
    part_blocks = seq_part.reshape(block_count, -1)
    term = jnp.dot(matched, part_blocks, preferred_element_type=jnp.float32)
    weight_grad = lax.psum_scatter(
        term.reshape(slot_rows * lax.axis_size("dp"), head_count * 2 * head_size).astype(
            jnp.bfloat16
        ),
        "dp",
        scatter_dimension=0,
        tiled=True,
    ).astype(jnp.float32)
    all_heads = lax.all_gather(pair_grad, "mp", axis=1, tiled=True)
    rows_all = lax.all_to_all(weights, "mp", split_axis=0, concat_axis=1, tiled=True)
    heads_flat = all_heads.reshape(tok_count, -1)
    rows_flat = rows_all.reshape(rows_all.shape[0], -1)
    input_grad = lax.dot_general(
        heads_flat, rows_flat, (((1,), (1,)), ((), ())), preferred_element_type=jnp.float32
    ).astype(jnp.bfloat16)
    return (input_grad, query_grad, weight_grad.reshape(slot_rows, head_count, 2, head_size))


def solution(mesh):
    return jax.shard_map(
        local,
        mesh=mesh,
        in_specs=(
            P("dp", None),
            P("dp", "mp", None),
            P("dp", "mp", None),
            P("dp", None),
            P("dp", "mp", None, None),
            P(),
            P(),
        ),
        out_specs=(P("dp", "mp"), P("dp", "mp", None), P("dp", "mp", None, None)),
        check_vma=False,
    )
```

profile of v0, /device:TPU:0, one launch (start us, length us, event | category | flops | bytes accessed | tf_op | source)
XLA Modules:
  0.0 885.2 jit_solution(16510195528750602497)
XLA Ops:
  7.2 3.6 copy.88
  10.9 7.5 copy.99
  18.4 7.6 copy.94
  27.3 154.5 %all-gather.3.cloned.1.call-done = bf16[16384,4,2,128]{3,1,2,0:T(4,128)(2,1)} async-done(((bf16[1024,4,2,128]{3,1,2,0:T(4,128)(2,1)}), bf16[16384,4,2,128]{3,1,2,0:T(4,128)(2,1)}) %all-gather.3.cloned.1.call-update) | async-done | bytes 33554448 | tf_op jit(solution)/shard_map/all_gather | solution.py:85
  181.8 64.4 %copy.89 = bf16[16384,4,2,128]{3,2,1,0:T(2,128)(2,1)} copy(bf16[16384,4,2,128]{3,1,2,0:T(4,128)(2,1)} %all-gather.3.cloned.1.call-done) | data formatting | bytes 67108864 | tf_op jit(solution)/shard_map/all_gather | solution.py:85
  246.2 34.5 %reshape.90 = bf16[128,131072]{1,0:T(8,128)(2,1)} reshape(bf16[16384,4,2,128]{3,2,1,0:T(2,128)(2,1)} %copy.89) | data formatting | bytes 67108864 | tf_op jit(solution)/shard_map/reshape | solution.py:70
  280.7 18.9 %convolution_convert_fusion.1 = bf16[64,131072]{1,0:T(8,128)(2,1)} fusion(bf16[128,131072]{1,0:T(8,128)(2,1)} %reshape.90, s32[64]{0:T(128)S(1)} %copy-done.6), kind=kOutput, calls=%fused_computation.2 | convolution fusion | flops 2155896832 | bytes 50331904 | tf_op jit(solution)/shard_map/dot_general | solution.py:71
  299.6 17.0 %reshape_reshape.3 = bf16[8192,1024]{1,0:T(8,128)(2,1)} reshape(bf16[64,131072]{1,0:T(8,128)(2,1)} %convolution_convert_fusion.1) | data formatting | bytes 33554432 | tf_op jit(solution)/shard_map/reshape;reshape | solution.py:18
  316.6 14.3 %fusion.31 = f32[1024,512]{1,0:T(8,128)S(1)} fusion(bf16[8192,1024]{1,0:T(8,128)(2,1)} %reshape_reshape.3, bf16[512,8192]{1,0:T(8,128)(2,1)} %param.7), kind=kOutput, calls=%fused_computation.57 | convolution fusion | flops 8589934592 | bytes 27262976 | tf_op jit(solution)/shard_map/dot_general | solution.py:16
  335.9 20.5 %fusion.30 = (f32[4,8,512]{2,1,0:T(8,128)S(1)}, f32[4,8,512,512]{2,3,1,0:T(8,128)}) fusion(pred[512,512]{0,1:T(8,128)(4,1)S(1)} %fusion.18, bf16[512,4,8,128]{0,3,2,1:T(8,128)(2,1)} %copy.99, bf16[512,4,64]{2,0,1:T(8,128)(2,1)} %get-tuple-element.19, bf16[512,4,64]{2,0,1:T(8,128)(2,1)} %get-tuple-element.18), kind=kOutput, calls=%fused_computation.56 | convolution fusion | flops 2182087168 | bytes 38600704 | tf_op jit(solution)/shard_map/sub | solution.py:43
  356.3 18.1 %fusion.7 = bf16[4,8,512,512]{2,3,1,0:T(8,128)(2,1)} fusion(f32[4,8,512,512]{2,3,1,0:T(8,128)} %get-tuple-element.27, f32[4,8,512]{2,1,0:T(8,128)S(1)} %get-tuple-element.26), kind=kLoop, calls=%fused_computation.14 | loop fusion | flops 16777216 | bytes 50397184 | tf_op jit(solution)/shard_map/convert_element_type | solution.py:45
  374.4 8.9 %convolution_bitcast_fusion = bf16[512,4,1,128]{3,0,1,2:T(8,128)(2,1)} fusion(bf16[4,8,512,512]{2,3,1,0:T(8,128)(2,1)} %fusion.7, bf16[512,4,8,128]{0,3,2,1:T(8,128)(2,1)S(1)} %bitcast.120), kind=kOutput, calls=%fused_computation.22 | convolution fusion | flops 2147483648 | bytes 21495808 | tf_op jit(solution)/shard_map/hgqk,qhgd->khd/dot_general | solution.py:57
  383.4 8.6 fusion.8
  392.0 25.1 %fusion.2 = bf16[4,8,512,512]{2,3,1,0:T(8,128)(2,1)} fusion(f32[4,8,512]{2,1,0:T(8,128)S(1)} %bitcast.129, f32[4,8,512,512]{2,3,1,0:T(8,128)} %get-tuple-element.27, f32[4,8,512]{2,1,0:T(8,128)S(1)} %get-tuple-element.26, bf16[512,4,8,128]{3,2,1,0:T(8,128)(2,1)} %bitcast.124, bf16[512,4,1,128]{3,0,1,2:T(8,128)(2,1)} %copy.132), kind=kOutput, calls=%fused_computation.5 | convolution fusion | flops 2181038080 | bytes 55181312 | tf_op jit(solution)/shard_map/qhgd,khd->hgqk/dot_general | solution.py:48
  417.1 9.4 %fusion.13 = f32[512,4,128]{2,0,1:T(8,128)S(1)} fusion(bf16[4,8,512,512]{2,3,1,0:T(8,128)(2,1)} %fusion.2, bf16[512,4,8,128]{0,3,2,1:T(8,128)(2,1)} %copy.99), kind=kOutput, calls=%fused_computation.25 | convolution fusion | flops 2147745792 | bytes 22020096 | tf_op jit(solution)/shard_map/hgqk,qhgd->khd/dot_general | solution.py:56
  428.4 1.7 copy.108
  430.1 15.1 %convert_bitcast_fusion = bf16[8192,1024]{0,1:T(8,128)(2,1)} fusion(bf16[512,1024]{0,1:T(8,128)(2,1)S(1)} %bitcast.128, bf16[512,8192]{1,0:T(8,128)(2,1)} %param.7), kind=kOutput, calls=%fused_computation.9 | convolution fusion | flops 8598323200 | bytes 26214400 | tf_op jit(solution)/shard_map/dot_general | solution.py:92
  445.2 22.4 %copy.109 = bf16[8192,1024]{1,0:T(8,128)(2,1)} copy(bf16[8192,1024]{0,1:T(8,128)(2,1)} %convert_bitcast_fusion) | data formatting | bytes 33554432 | tf_op jit(solution)/shard_map/convert_element_type | solution.py:94
  467.6 17.0 %reshape.97 = bf16[64,131072]{1,0:T(8,128)(2,1)} reshape(bf16[8192,1024]{1,0:T(8,128)(2,1)} %copy.109) | data formatting | bytes 33554432 | tf_op jit(solution)/shard_map/reshape | solution.py:97
  484.6 23.0 %convolution_convert_fusion = bf16[128,131072]{1,0:T(8,128)(2,1)} fusion(bf16[64,131072]{1,0:T(8,128)(2,1)} %reshape.97, s32[64]{0:T(128)S(1)} %copy-done.5), kind=kOutput, calls=%fused_computation.1 | convolution fusion | flops 2164269056 | bytes 50331904 | tf_op jit(solution)/shard_map/dot_general | solution.py:98
  507.6 33.2 %convert_element_type.77 = bf16[16384,1024]{1,0:T(8,128)(2,1)} reshape(bf16[128,131072]{1,0:T(8,128)(2,1)} %convolution_convert_fusion) | data formatting | bytes 67108864 | tf_op jit(solution)/shard_map/convert_element_type | solution.py:100
  540.9 21.3 %reshape.95 = bf16[8192,4,2,128]{3,2,1,0:T(2,128)(2,1)} reshape(bf16[64,131072]{1,0:T(8,128)(2,1)} %convolution_convert_fusion.1) | data formatting | bytes 33554432 | tf_op jit(solution)/shard_map/reshape | solution.py:89
  562.2 12.9 %all-to-all-start = ((bf16[8192,4,2,128]{3,2,1,0:T(2,128)(2,1)}), bf16[8192,4,2,128]{3,2,1,0:T(2,128)(2,1)}, u32[]{:S(2)}, u32[]{:S(2)}) async-start(bf16[8192,4,2,128]{3,2,1,0:T(2,128)(2,1)} %reshape.95), calls=%async_computation | async-start | bytes 33554432 | tf_op jit(solution)/shard_map/all_to_all | solution.py:108
  575.2 13.7 %multiply_convert_fusion = bf16[4,128,8,512]{3,1,2,0:T(8,128)(2,1)} fusion(bf16[4,8,512,512]{2,3,1,0:T(8,128)(2,1)} %fusion.2, bf16[512,4,64]{2,0,1:T(8,128)(2,1)S(1)} %copy-done.2, bf16[512,4,64]{2,0,1:T(8,128)(2,1)S(1)} %copy-done.1), kind=kOutput, calls=%fused_computation.17 | convolution fusion | flops 2152726528 | bytes 21495808 | tf_op jit(solution)/shard_map/hgqk,khd->qhgd/dot_general | solution.py:52
  588.9 7.9 copy.110
  596.8 2.9 copy.103
  599.6 158.1 %all-to-all-done = bf16[8192,4,2,128]{3,2,1,0:T(2,128)(2,1)} async-done(((bf16[8192,4,2,128]{3,2,1,0:T(2,128)(2,1)}), bf16[8192,4,2,128]{3,2,1,0:T(2,128)(2,1)}, u32[]{:S(2)}, u32[]{:S(2)}) %all-to-all-start) | async-done | bytes 16777248 | tf_op jit(solution)/shard_map/all_to_all | solution.py:108
  757.7 15.1 %copy.104 = bf16[8192,4,2,128]{3,0,2,1:T(8,128)(2,1)} copy(bf16[8192,4,2,128]{3,2,1,0:T(2,128)(2,1)} %all-to-all-done) | data formatting | bytes 33554432 | tf_op jit(solution)/shard_map/all_to_all | solution.py:108
  772.9 20.8 %copy.105 = bf16[4096,2,4,2,128]{0,4,3,2,1:T(8,128)(2,1)} copy(bf16[4096,2,4,2,128]{4,0,1,3,2:T(8,128)(2,1)} %bitcast.118) | data formatting | bytes 33554432 | tf_op jit(solution)/shard_map/all_to_all | solution.py:108
  793.7 13.9 %convolution_convert_fusion.2 = bf16[512,4096]{1,0:T(8,128)(2,1)} fusion(bf16[512,2048]{0,1:T(8,128)(2,1)S(1)} %bitcast.125, bf16[4096,2048]{0,1:T(8,128)(2,1)} %bitcast.119), kind=kOutput, calls=%fused_computation.18 | convolution fusion | flops 8592031744 | bytes 23068672 | tf_op jit(solution)/shard_map/dot_general | solution.py:111
  807.5 64.1 %reduce-scatter.2.cloned.1.call-done = bf16[1024,1024]{1,0:T(8,128)(2,1)} async-done(((bf16[16384,1024]{1,0:T(8,128)(2,1)}), bf16[1024,1024]{1,0:T(8,128)(2,1)}) %reduce-scatter.2.cloned.1.call-update) | async-done | bytes 2097168 | tf_op jit(solution)/shard_map/reduce_scatter | solution.py:99
  871.7 6.6 reshape.101
  (33 shorter events, 8.2 us)
Async XLA Ops:
  7.2 18.9 %copy-start.4 = (s32[1,512]{1,0:T(1,128)S(1)}, s32[1,512]{1,0:T(1,128)}, u32[]{:S(2)}) copy-start(s32[1,512]{1,0:T(1,128)} %param.10) | copy-start | bytes 6148
  7.2 174.6 %all-gather.3.cloned.1.call-start = ((), (), s32[]{:S(2)}) async-start(), calls=%async_computation.2 | async-start | bytes 35651584 | tf_op jit(solution)/shard_map/all_gather | solution.py:85
  10.9 585.9 %all-gather.5.cloned.1.call-start = ((), (), s32[]{:S(2)}) async-start(), calls=%async_computation.3 | async-start | bytes 3145728 | tf_op jit(solution)/shard_map/all_gather | solution.py:107
  246.2 34.5 %copy-start.6 = (s32[64]{0:T(128)S(1)}, s32[64]{0:T(128)}, u32[]{:S(2)}) copy-start(s32[64]{0:T(128)} %param.12) | copy-start | bytes 772
  356.3 18.1 %copy-start = (bf16[512,32,128]{0,2,1:T(8,128)(2,1)S(1)}, bf16[512,32,128]{0,2,1:T(8,128)(2,1)}, u32[]{:S(2)}) copy-start(bf16[512,32,128]{0,2,1:T(8,128)(2,1)} %copy.94) | copy-start | bytes 12582916
  417.1 10.1 %copy-start.3 = (bf16[512,4,1,128]{3,0,1,2:T(8,128)(2,1)S(1)}, bf16[512,4,1,128]{3,0,1,2:T(8,128)(2,1)}, u32[]{:S(2)}) copy-start(bf16[512,4,1,128]{3,0,1,2:T(8,128)(2,1)} %convolution_bitcast_fusion) | copy-start | bytes 1572868
  428.3 443.3 %reduce-scatter.2.cloned.1.call-start = ((), (), s32[]{:S(2)}) async-start(), calls=%async_computation.4 | async-start | bytes 35651584 | tf_op jit(solution)/shard_map/reduce_scatter | solution.py:99
  467.6 17.0 %copy-start.5 = (s32[64]{0:T(128)S(1)}, s32[64]{0:T(128)}, u32[]{:S(2)}) copy-start(s32[64]{0:T(128)} %param.13) | copy-start | bytes 772
  562.2 12.9 %copy-start.1 = (bf16[512,4,64]{2,0,1:T(8,128)(2,1)S(1)}, bf16[512,4,64]{2,0,1:T(8,128)(2,1)}, u32[]{:S(2)}) copy-start(bf16[512,4,64]{2,0,1:T(8,128)(2,1)} %get-tuple-element.18) | copy-start | bytes 786436
  562.2 12.9 %copy-start.2 = (bf16[512,4,64]{2,0,1:T(8,128)(2,1)S(1)}, bf16[512,4,64]{2,0,1:T(8,128)(2,1)}, u32[]{:S(2)}) copy-start(bf16[512,4,64]{2,0,1:T(8,128)(2,1)} %get-tuple-element.19) | copy-start | bytes 786436
  562.2 195.5 %all-to-all-start = ((bf16[8192,4,2,128]{3,2,1,0:T(2,128)(2,1)}), bf16[8192,4,2,128]{3,2,1,0:T(2,128)(2,1)}, u32[]{:S(2)}, u32[]{:S(2)}) async-start(bf16[8192,4,2,128]{3,2,1,0:T(2,128)(2,1)} %reshape.95), calls=%async_computation | async-start | bytes 33554432 | tf_op jit(solution)/shard_map/all_to_all | solution.py:108
Sparse Core Ops, SparseCore 0:
  11.0 170.7 all-gather.2
  428.4 33.0 all-gather.4
  541.0 330.5 reduce-scatter.1
where the time goes:
time: 897 us; the launch traced here: 885 us
  waiting for transfers between devices  377 us (42%)
  local copies, waits for them, and re-layouts  287 us (32%)
  matrix products  171 us (19%)
  other arithmetic  22.4 us (2%)
  between operations  14.3 us (2%)
  starting transfers between devices  13 us (1%)
    all_to_all x1, waiting for transfers between devices, local(): lax.all_to_all(weights, 'mp', split_axis=0, concat_axis=1, tiled=True)  158 us
    all_gather x1, waiting for transfers between devices, local(): gathered = lax.all_gather(weight_slots, 'dp', axis=0, tiled=True)  155 us
    all_gather x1, local copies, waits for them, and re-layouts, local(): gathered = lax.all_gather(weight_slots, 'dp', axis=0, tiled=True)  64.4 us
    reduce_scatter x1, waiting for transfers between devices, local(): lax.psum_scatter(term.reshape(slot_rows * lax.axis_size('dp'), head_count...  64.1 us
    all_to_all x2, local copies, waits for them, and re-layouts, local(): lax.all_to_all(weights, 'mp', split_axis=0, concat_axis=1, tiled=True)  36 us
    reshape x1, local copies, waits for them, and re-layouts, pick_blocks(): flat = source.reshape(block_total, -1)  34.5 us
    convert_element_type x1, local copies, waits for them, and re-layouts, local(): term.reshape(slot_rows * lax.axis_size('dp'), head_count * 2 * head_size)  33.2 us
    dot_general x1, matrix products, attend(): prob_grad = jnp.einsum('qhgd,khd->hgqk', outgrad_wide, value_wide)  25.1 us
  transfers between devices with their start and end apart: 4, of which 3 were waited for; matrix products, arithmetic and copies ran while one was open for 25% of the time, Pallas kernels for 0%

commit v1 on v0

v1 whole, which is shorter than its diff:
```python
import functools

import jax
import jax.numpy as jnp
from jax import lax
from jax.experimental import pallas as pl
from jax.experimental.pallas import tpu as pltpu
from jax.sharding import PartitionSpec as P

BR = 128
QT = 128
REACH = 2
NEG = -1e30


def attn_kernel(proj_ref, cos_ref, sin_ref, segc_ref, segr_ref, q_ref, g_ref, dq_ref, pair_ref, k_s, kt_s, v_s, bias_s, dk_s, dv_s):
    tok, hd = k_s.shape
    per_head = q_ref.shape[1] // hd
    tiles = tok // QT
    inv_root = hd ** -0.5
    scale = inv_root * 1.4426950408889634
    f32, bf16 = jnp.float32, jnp.bfloat16

    raw = proj_ref[:, :hd]
    keys = (raw * cos_ref[...] + pltpu.roll(raw, hd // 2, 1) * sin_ref[...]).astype(bf16)
    k_s[...] = keys
    kt_s[...] = keys.astype(f32).T.astype(bf16)
    v_s[...] = proj_ref[:, hd:].astype(bf16)
    dk_s[...] = jnp.zeros_like(dk_s)
    dv_s[...] = jnp.zeros_like(dv_s)
    for t in range(tiles):
        k0 = max(0, t - REACH) * QT
        k1 = (t + 1) * QT
        same = segc_ref[k0:k1, :] == segr_ref[0:1, t * QT:(t + 1) * QT]
        kpos = lax.broadcasted_iota(jnp.int32, (k1 - k0, QT), 0) + k0
        qpos = lax.broadcasted_iota(jnp.int32, (k1 - k0, QT), 1) + t * QT
        bias_s[t, 0:k1 - k0, :] = jnp.where(same & (kpos <= qpos), 0.0, NEG)

    def two_heads(hp, carry):
        c0 = pl.multiple_of(hp * 2 * hd, hd)
        c1 = pl.multiple_of(hp * 2 * hd + hd, hd)
        for t in range(tiles):
            k0 = max(0, t - REACH) * QT
            k1 = (t + 1) * QT
            rows = pl.ds(t * QT, QT)
            q2 = jnp.concatenate([q_ref[rows, pl.ds(c0, hd)], q_ref[rows, pl.ds(c1, hd)]], axis=0)
            g2 = jnp.concatenate([g_ref[rows, pl.ds(c0, hd)], g_ref[rows, pl.ds(c1, hd)]], axis=0)
            nt = (((1,), (1,)), ((), ()))
            bias = bias_s[t, 0:k1 - k0, :]
            bias = jnp.concatenate([bias, bias], axis=1)
            s = lax.dot_general(k_s[k0:k1, :], q2, nt, preferred_element_type=f32) * scale + bias
            e = jnp.exp2(s - jnp.max(s, axis=0, keepdims=True))
            p = e * (1.0 / jnp.sum(e, axis=0, keepdims=True))
            pb = p.astype(bf16)
            dp = lax.dot_general(v_s[k0:k1, :], g2, nt, preferred_element_type=f32)
            rd = jnp.sum(pb.astype(f32) * dp, axis=0, keepdims=True)
            ds = (p * (dp - rd)).astype(bf16)
            dv_s[k0:k1, :] += jnp.dot(pb, g2, preferred_element_type=f32)
            dk_s[k0:k1, :] += jnp.dot(ds, q2, preferred_element_type=f32)
            dqt = jnp.dot(kt_s[:, k0:k1], ds, preferred_element_type=f32) * inv_root
            dq_ref[rows, pl.ds(c0, hd)] = dqt[:, :QT].T.astype(bf16)
            dq_ref[rows, pl.ds(c1, hd)] = dqt[:, QT:].T.astype(bf16)
        return carry

    lax.fori_loop(0, per_head // 2, two_heads, 0)
    rot = dk_s[...] * inv_root
    pair_ref[:, :hd] = (rot * cos_ref[...] - pltpu.roll(rot, hd // 2, 1) * sin_ref[...]).astype(bf16)
    pair_ref[:, hd:] = dv_s[...].astype(bf16)


def attention(proj, cos, sin, segc, segr, q2d, g2d, hd, head0=0):
    tok = proj.shape[0]
    heads = proj.shape[1] // (2 * hd)
    total = q2d.shape[1] // hd
    return functools.partial(_attention, tok, heads, hd, head0)(proj, cos, sin, segc, segr, q2d, g2d)


def _attention(tok, heads, hd, head0, proj, cos, sin, segc, segr, q2d, g2d, per_head=8):
    wide = per_head * hd
    full = lambda a: pl.BlockSpec(a.shape, lambda i: (0, 0))
    col = lambda w, off=0: pl.BlockSpec((tok, w), lambda i: (0, i + off))
    tiles = tok // QT
    span = min(REACH + 1, tiles) * QT
    work = tok * span * heads * per_head
    return pl.pallas_call(
        attn_kernel,
        grid=(heads,),
        in_specs=[col(2 * hd), full(cos), full(sin), full(segc), full(segr), col(wide, head0), col(wide, head0)],
        out_specs=[col(wide), col(2 * hd)],
        out_shape=[
            jax.ShapeDtypeStruct((tok, heads * wide), jnp.bfloat16),
            jax.ShapeDtypeStruct((tok, heads * 2 * hd), jnp.bfloat16),
        ],
        scratch_shapes=[
            pltpu.VMEM((tok, hd), jnp.bfloat16),
            pltpu.VMEM((hd, tok), jnp.bfloat16),
            pltpu.VMEM((tok, hd), jnp.bfloat16),
            pltpu.VMEM((tiles, span, QT), jnp.float32),
            pltpu.VMEM((tok, hd), jnp.float32),
            pltpu.VMEM((tok, hd), jnp.float32),
        ],
        cost_estimate=pl.CostEstimate(flops=10 * work * hd, bytes_accessed=6 * tok * heads * wide, transcendentals=work),
        name="attn",
    )(proj, cos, sin, segc, segr, q2d, g2d)


def rope_tables(tok, hd):
    frequency = 500000.0 ** (-2.0 * jnp.arange(hd // 2, dtype=jnp.float32) / hd)
    angle = jnp.arange(tok, dtype=jnp.float32)[:, None] * frequency[None, :]
    cos, sin = jnp.cos(angle), jnp.sin(angle)
    return jnp.concatenate([cos, cos], axis=1), jnp.concatenate([-sin, sin], axis=1)


def seg_tables(seg_row):
    tok = seg_row.shape[0]
    return jnp.broadcast_to(seg_row[:, None], (tok, 128)), jnp.broadcast_to(seg_row[None, :], (8, tok))


def local(tokens, queries, out_grad, segment_ids, weight_slots, old_place, new_place):
    tok = tokens.shape[0]
    slot_rows, heads, _, hd = weight_slots.shape
    wide = heads * 2 * hd
    slot_total = lax.axis_size("dp") * (slot_rows // BR)
    blocks = old_place.shape[0]
    q2d = queries.reshape(tok, -1)
    g2d = out_grad.reshape(tok, -1)
    cos, sin = rope_tables(tok, hd)
    segc, segr = seg_tables(segment_ids[0])

    gathered = lax.all_gather(weight_slots.reshape(slot_rows, wide), "dp", axis=0, tiled=True)
    weights = jnp.take(gathered.reshape(slot_total, BR, wide), old_place, axis=0, mode="clip").reshape(blocks * BR, wide)
    proj = jnp.dot(tokens, weights, preferred_element_type=jnp.float32)
    dq, pair = attention(proj, cos, sin, segc, segr, q2d, g2d, hd)

    seq_part = lax.dot_general(tokens, pair, (((0,), (0,)), ((), ())), preferred_element_type=jnp.float32).astype(jnp.bfloat16)
    hit = new_place[None, :] == jnp.arange(slot_total, dtype=jnp.int32)[:, None]
    slot_block = jnp.max(jnp.where(hit, jnp.arange(blocks, dtype=jnp.int32)[None, :], -1), axis=1)
    spread = jnp.take(seq_part.reshape(blocks, BR, wide), jnp.maximum(slot_block, 0), axis=0, mode="clip")
    spread = jnp.where((slot_block >= 0)[:, None, None], spread, 0)
    weight_grad = lax.psum_scatter(spread.reshape(slot_total * BR, wide), "dp", scatter_dimension=0, tiled=True)

    part = lax.dot_general(pair, weights, (((1,), (1,)), ((), ())), preferred_element_type=jnp.float32).astype(jnp.bfloat16)
    input_grad = lax.psum_scatter(part, "mp", scatter_dimension=1, tiled=True)
    return (
        input_grad,
        dq.reshape(queries.shape),
        weight_grad.astype(jnp.float32).reshape(slot_rows, heads, 2, hd),
    )


def solution(mesh):
    return jax.shard_map(
        local,
        mesh=mesh,
        in_specs=(
            P("dp", None),
            P("dp", "mp", None),
            P("dp", "mp", None),
            P("dp", None),
            P("dp", "mp", None, None),
            P(),
            P(),
        ),
        out_specs=(P("dp", "mp"), P("dp", "mp", None), P("dp", "mp", None, None)),
        check_vma=False,
    )
```

time: 897 us -> 767 us (0.86); the launches traced: 885 us -> 766 us
  local copies, waits for them, and re-layouts: 287 us -> 86.4 us
  waiting for transfers between devices: 377 us -> 541 us
  matrix products: 171 us -> 61.1 us
  Pallas kernels: 0 us -> 37.3 us
  starting transfers between devices: 13 us -> 0.12 us
    reduce_scatter x1 -> x2, waiting for transfers between devices: 64.1 us -> 387 us  [the longest x1 293 us: local(): lax.psum_scatter(spread.reshape(slot_total * BR, wide), 'dp', scatter_dim...]
    all_to_all x1 -> x0, waiting for transfers between devices: 158 us -> none  [local(): lax.all_to_all(weights, 'mp', split_axis=0, concat_axis=1, tiled=True)]
    dot_general x10 -> x3, matrix products: 151 us -> 61.1 us  [the longest x1 30.3 us: local(): lax.dot_general(pair, weights, (((1,), (1,)), ((), ())), preferred_elemen...]
    all_gather x2 -> x0, local copies, waits for them, and re-layouts: 67.3 us -> none  [the longest x1 64.4 us: local(): gathered = lax.all_gather(weight_slots, 'dp', axis=0, tiled=True)]
    convert_element_type x3 -> x0, local copies, waits for them, and re-layouts: 57.4 us -> none  [the longest x1 33.2 us: local(): term.reshape(slot_rows * lax.axis_size('dp'), head_count * 2 * head_size)]
    reshape x5 -> x4, local copies, waits for them, and re-layouts: 87 us -> 46.7 us  [the longest x1 22.4 us: local(): seq_part.reshape(blocks, BR, wide)]
    pallas_call x0 -> x1, Pallas kernels: none -> 37.3 us  [_attention(): pl.pallas_call(attn_kernel, grid=(heads,), in_specs=[col(2 * hd), full(co...]
    all_to_all x2 -> x0, local copies, waits for them, and re-layouts: 36 us -> none  [local(): lax.all_to_all(weights, 'mp', split_axis=0, concat_axis=1, tiled=True)]
  transfers between devices with their start and end apart: 4 -> 3, of which waited for: 3 -> 3; matrix products, arithmetic and copies ran while one was open for 25% -> 8% of each run, Pallas kernels for 0% -> 0%
where the time goes in v1:
time: 767 us; the launch traced here: 766 us
  waiting for transfers between devices  541 us (71%)
  local copies, waits for them, and re-layouts  86.4 us (11%)
  matrix products  61.1 us (8%)
  Pallas kernels  37.3 us (5%)
  other arithmetic  26.3 us (3%)
  between operations  13.8 us (2%)
    reduce_scatter x1, waiting for transfers between devices, local(): lax.psum_scatter(spread.reshape(slot_total * BR, wide), 'dp', scatter_dim...  293 us
    all_gather x1, waiting for transfers between devices, local(): lax.all_gather(weight_slots.reshape(slot_rows, wide), 'dp', axis=0, tiled...  154 us
    reduce_scatter x1, waiting for transfers between devices, local(): input_grad = lax.psum_scatter(part, 'mp', scatter_dimension=1, tiled=True)  94.7 us
    pallas_call x1, Pallas kernels, _attention(): pl.pallas_call(attn_kernel, grid=(heads,), in_specs=[col(2 * hd), full(co...  37.3 us
    dot_general x1, matrix products, local(): lax.dot_general(pair, weights, (((1,), (1,)), ((), ())), preferred_elemen...  30.3 us
    select_n x1, other arithmetic, local(): spread = jnp.where((slot_block >= 0)[:, None, None], spread, 0)  22.9 us
    reshape x1, local copies, waits for them, and re-layouts, local(): seq_part.reshape(blocks, BR, wide)  22.4 us
    gather x1, local copies, waits for them, and re-layouts, local(): jnp.take(seq_part.reshape(blocks, BR, wide), jnp.maximum(slot_block, 0),...  18.5 us
  transfers between devices with their start and end apart: 3, of which 3 were waited for; matrix products, arithmetic and copies ran while one was open for 8% of the time, Pallas kernels for 0%

profile of v1, /device:TPU:0, one launch (start us, length us, event | category | flops | bytes accessed | tf_op | source)
XLA Modules:
  0.0 766.4 jit_solution(2172945766429461903)
XLA Ops:
  7.2 0.0 all-gather.2.cloned.1.call-start
  7.2 4.4 reshape.55
  11.6 0.0 all-gather.2.cloned.1.call-update
  11.7 0.0 reduce-scatter.5.cloned.1.call-start
  11.7 0.7 select_reduce_fusion
  12.5 0.7 pad_clamp_fusion.1
  13.2 1.0 fusion.2
  14.2 1.0 pad_maximum_fusion
  15.2 0.1 broadcast_bitcast_fusion
  15.3 13.2 %copy_bitcast_fusion = (bf16[512,4096]{1,0:T(8,128)(2,1)}, bf16[512,4096]{1,0:T(8,128)(2,1)}) fusion(bf16[64,8,32,128]{3,2,1,0:T(8,128)(2,1)} %bitcast.32, bf16[64,8,32,128]{3,2,1,0:T(8,128)(2,1)} %bitcast.33), kind=kLoop, calls=%fused_computation.5 | loop fusion | bytes 16777216 | tf_op jit(solution)/shard_map/reshape | solution.py:126
  28.5 154.1 %all-gather.2.cloned.1.call-done = bf16[16384,1024]{1,0:T(8,128)(2,1)} async-done(((bf16[1024,1024]{1,0:T(8,128)(2,1)}), bf16[16384,1024]{1,0:T(8,128)(2,1)}) %all-gather.2.cloned.1.call-update) | async-done | bytes 33554448 | tf_op jit(solution)/shard_map/all_gather | solution.py:130
  182.6 11.9 %gather_fusion = bf16[64,128,1024]{2,1,0:T(8,128)(2,1)} fusion(bf16[128,128,1024]{2,1,0:T(8,128)(2,1)} %bitcast.29, s32[1024]{0:T(1024)S(1)} %pad_clamp_fusion.1), kind=kCustom, calls=%fused_computation | custom fusion | bytes 33554688 | tf_op jit(solution)/shard_map/jit(_take)/gather | solution.py:131
  194.5 0.0 copy-start
  194.5 15.7 %convolution_bitcast_fusion.proj_ref = f32[512,1024]{1,0:T(8,128)} fusion(bf16[512,8192]{1,0:T(8,128)(2,1)} %param.7, bf16[8192,1024]{1,0:T(8,128)(2,1)} %bitcast.27), kind=kOutput, calls=%fused_computation.7 | convolution fusion | flops 8589934592 | bytes 27262976 | tf_op jit(solution)/shard_map/dot_general | solution.py:132
  210.2 0.0 copy-done
  210.2 0.6 broadcast_in_dim.55.segr_ref
  210.8 0.8 broadcast_in_dim.54.segc_ref
  211.7 37.3 %attn.1 = (bf16[512,4096]{1,0:T(8,128)(2,1)}, bf16[512,1024]{1,0:T(8,128)(2,1)}) custom-call(f32[512,1024]{1,0:T(8,128)} %convolution_bitcast_fusion.proj_ref, f32[512,128]{1,0:T(8,128)} %get-tuple-element.10.cos_ref, f32[512,128]{1,0:T(8,128)} %get-tuple-element.11.sin_ref, s32[512,128]{1,0:T(8,128)} %broadcast_in_dim.54.segc_ref, ...), custom_call_target="tpu_custom_call" | custom-call | flops 8053063680 | bytes 12582912 | tf_op jit(solution)/shard_map/attn/pallas_call | solution.py:85
  249.0 15.1 %convert_bitcast_fusion = bf16[8192,1024]{0,1:T(8,128)(2,1)} fusion(bf16[512,1024]{1,0:T(8,128)(2,1)} %get-tuple-element.5, bf16[512,8192]{1,0:T(8,128)(2,1)} %param.7), kind=kOutput, calls=%fused_computation.3 | convolution fusion | flops 8598323200 | bytes 26214400 | tf_op jit(solution)/shard_map/dot_general | solution.py:135
  264.1 22.4 %copy.17 = bf16[8192,1024]{1,0:T(8,128)(2,1)} copy(bf16[8192,1024]{0,1:T(8,128)(2,1)} %convert_bitcast_fusion) | data formatting | bytes 33554432 | tf_op jit(solution)/shard_map/reshape | solution.py:138
  286.5 18.5 %gather_fusion.1 = bf16[128,128,1024]{2,1,0:T(8,128)(2,1)} fusion(bf16[64,128,1024]{2,1,0:T(8,128)(2,1)} %bitcast.26, s32[1024]{0:T(1024)S(1)} %pad_clamp_fusion), kind=kCustom, calls=%fused_computation.1 | custom fusion | bytes 67109376 | tf_op jit(solution)/shard_map/jit(_take)/gather | solution.py:138
  305.0 22.9 %bitcast_select_fusion = bf16[16384,1024]{1,0:T(8,128)(2,1)} fusion(bf16[128,128,1024]{2,1,0:T(8,128)(2,1)} %gather_fusion.1, pred[16384]{0:T(1024)(128)(4,1)S(1)} %broadcast_bitcast_fusion), kind=kLoop, calls=%fused_computation.2 | loop fusion | flops 16777216 | bytes 67125248 | tf_op jit(solution)/shard_map/jit(_where)/select_n | solution.py:139
  327.9 0.0 copy-start.1
  327.9 0.0 reduce-scatter.5.cloned.1.call-update
  327.9 0.0 reduce-scatter.3.cloned.1.call-start
  327.9 1.1 copy-done.1
  329.1 30.3 %convolution_convert_fusion = bf16[512,8192]{1,0:T(8,128)(2,1)} fusion(bf16[512,1024]{1,0:T(8,128)(2,1)S(1)} %copy-done.1, bf16[8192,1024]{1,0:T(8,128)(2,1)} %bitcast.28), kind=kOutput, calls=%fused_computation.4 | convolution fusion | flops 8594128896 | bytes 26214400 | tf_op jit(solution)/shard_map/dot_general | solution.py:142
  359.4 0.0 reduce-scatter.3.cloned.1.call-update
  359.4 6.6 copy.20
  366.0 292.6 %reduce-scatter.5.cloned.1.call-done = bf16[1024,1024]{1,0:T(8,128)(2,1)} async-done(((bf16[16384,1024]{1,0:T(8,128)(2,1)}), bf16[1024,1024]{1,0:T(8,128)(2,1)}) %reduce-scatter.5.cloned.1.call-update) | async-done | bytes 2097168 | tf_op jit(solution)/shard_map/reduce_scatter | solution.py:140
  658.6 6.6 reshape.65
  665.1 94.7 %reduce-scatter.3.cloned.1.call-done = bf16[512,4096]{1,0:T(8,128)(2,1)} async-done(((bf16[512,8192]{1,0:T(8,128)(2,1)}), bf16[512,4096]{1,0:T(8,128)(2,1)}) %reduce-scatter.3.cloned.1.call-update) | async-done | bytes 4194320 | tf_op jit(solution)/shard_map/reduce_scatter | solution.py:143
  (4 shorter events, 0.0 us)
Async XLA Ops:
  7.2 175.4 %all-gather.2.cloned.1.call-start = ((), (), s32[]{:S(2)}) async-start(), calls=%async_computation.2 | async-start | bytes 35651584 | tf_op jit(solution)/shard_map/all_gather | solution.py:130
  11.7 646.9 %reduce-scatter.5.cloned.1.call-start = ((), (), s32[]{:S(2)}) async-start(), calls=%async_computation.4 | async-start | bytes 35651584 | tf_op jit(solution)/shard_map/reduce_scatter | solution.py:140
  194.5 15.7 %copy-start = (s32[1,512]{1,0:T(1,128)S(1)}, s32[1,512]{1,0:T(1,128)}, u32[]{:S(2)}) copy-start(s32[1,512]{1,0:T(1,128)} %param.10) | copy-start | bytes 6148
  327.9 1.2 copy-start.1
  327.9 432.0 %reduce-scatter.3.cloned.1.call-start = ((), (), s32[]{:S(2)}) async-start(), calls=%async_computation.3 | async-start | bytes 12582912 | tf_op jit(solution)/shard_map/reduce_scatter | solution.py:143
Sparse Core Ops, SparseCore 0:
  11.8 170.7 all-gather.1
  328.0 330.4 reduce-scatter.4
  661.4 98.3 reduce-scatter.2
